TPU v7x, 512 devices: a whole 4x8x8 slice. The times are simulated.
512 devices in a mesh: dp: 2 (over core), row: 8 (over x, z_hi), col: 32 (over y, z_lo).
Axes of the slice: x: 4, y: 8, z: 8 (z_hi: 2, z_lo: 4; z = z_hi * 4 + z_lo), core: 2. Of those that a mesh axis runs over, the one named last changes fastest.
Arguments:
- hidden: bfloat16 [2048, 28672], P(('dp', 'row'), 'col'), may hold values from -0.125 to 0.125
- upstream: bfloat16 [2048, 8192], P('col', ('dp', 'row')), may hold values from -6 to 6
- weight: bfloat16 [28672, 8192], P('col', ('dp', 'row')), may hold values from -0.03125 to 0.03125
Outputs:
- input_grad: bfloat16 [2048, 28672], P(('dp', 'row'), 'col')
- weight_grad: float32 [28672, 8192], P('col', ('dp', 'row'))
All inputs are finite; a program needn't handle non-finite values.
Results may differ from a plain program's by a relative error of at most 0.014.
Values may be sent and summed in bfloat16 or wider, within the bound.
A program may use at most 64 MiB of HBM per device.

v0:
```python
import jax
import jax.numpy as jnp
from jax import lax
from jax.sharding import Mesh
from jax.sharding import PartitionSpec as P

DP_ROW = ("dp", "row_0", "row_1")


def sent_to_all(value, axis):
    copies = jnp.broadcast_to(value, (lax.axis_size(axis), *value.shape))
    return lax.all_to_all(copies, axis, split_axis=0, concat_axis=0, tiled=True)


def joined_along(parts, dim):
    parts = jnp.moveaxis(parts, 0, dim)
    shape = parts.shape
    return parts.reshape(*shape[:dim], shape[dim] * shape[dim + 1], *shape[dim + 2 :])


def gather_directly(value, axis, dim):
    parts = sent_to_all(value, axis)
    return joined_along(parts, dim)


def own_rows(terms, axes):
    running = terms.astype(jnp.bfloat16)
    for axis in axes:
        running = lax.psum_scatter(running, axis, scatter_dimension=0, tiled=True)
    return running.astype(jnp.float32)


def local(hidden, upstream, weight):
    gathered = gather_directly(upstream, "col", 0)
    picked = gathered
    weight_grad = lax.dot_general(
        lax.all_gather(hidden, DP_ROW, axis=0, tiled=True),
        picked,
        (((0,), (0,)), ((), ())),
        preferred_element_type=jnp.float32,
    )
    picked = gathered
    summed = own_rows(
        lax.dot_general(
            picked, weight, (((1,), (1,)), ((), ())), preferred_element_type=jnp.float32
        ),
        DP_ROW,
    )
    return (summed.astype(jnp.bfloat16), weight_grad)


def solution(mesh):
    finer = Mesh(
        mesh.devices.reshape(mesh.shape["dp"], 4, 2, mesh.shape["col"]),
        ("dp", "row_0", "row_1", "col"),
    )
    placed = (P(DP_ROW, "col"), P("col", DP_ROW), P("col", DP_ROW))
    return jax.shard_map(
        local,
        mesh=finer,
        in_specs=placed,
        out_specs=(P(DP_ROW, "col"), P("col", DP_ROW)),
        check_vma=False,
    )
```

profile of v0, /device:TPU:129, one launch (start us, length us, event | category | flops | bytes accessed | tf_op | source)
XLA Modules:
  0.0 199.5 jit_solution(16656601850592454004)
XLA Ops:
  8.0 0.0 copy-start
  8.0 0.0 reduce-scatter.4.cloned.1.call-start
  8.1 1.1 broadcast_in_dim.3
  9.2 60.3 %all_to_all.5 = bf16[32,64,512]{2,1,0:T(8,128)(2,1)S(1)} all-to-all(bf16[32,64,512]{2,1,0:T(8,128)(2,1)S(1)} %broadcast_in_dim.3), channel_id=1, replica_groups=mesh['dp'=2,'row_0'=4,'row_1'=2,'col'=32] {'col'}, dimensions={0} | all-to-all | bytes 4194304 | tf_op jit(solution)/shard_map/all_to_all | solution.py:12
  69.5 0.0 copy-done
  69.5 4.2 %convolution_convert_fusion = bf16[2048,896]{1,0:T(8,128)(2,1)} fusion(bf16[2048,512]{1,0:T(8,128)(2,1)S(1)} %bitcast.5, bf16[896,512]{1,0:T(8,128)(2,1)S(1)} %copy-done), kind=kOutput, calls=%fused_computation | convolution fusion | flops 1880883200 | bytes 6684672 | tf_op jit(solution)/shard_map/dot_general | solution.py:44
  73.7 0.0 reduce-scatter.4.cloned.1.call-update
  73.7 0.0 reduce-scatter.6.cloned.1.call-start
  73.7 21.6 %reduce-scatter.4.cloned.1.call-done = bf16[1024,896]{1,0:T(8,128)(2,1)} async-done(((bf16[2048,896]{1,0:T(8,128)(2,1)}), bf16[1024,896]{1,0:T(8,128)(2,1)}) %reduce-scatter.4.cloned.1.call-update) | async-done | bytes 1835024 | tf_op jit(solution)/shard_map/reduce_scatter | solution.py:29
  95.4 0.0 reduce-scatter.6.cloned.1.call-update
  95.4 0.0 all-gather.2.cloned.1.call-start
  95.5 0.5 all-gather.2.cloned.1.call-update
  96.0 0.0 reduce-scatter.8.cloned.1.call-start
  96.0 38.8 %reduce-scatter.6.cloned.1.call-done = bf16[256,896]{1,0:T(8,128)(2,1)} async-done(((bf16[1024,896]{1,0:T(8,128)(2,1)}), bf16[256,896]{1,0:T(8,128)(2,1)}) %reduce-scatter.6.cloned.1.call-update) | async-done | bytes 458768 | tf_op jit(solution)/shard_map/reduce_scatter | solution.py:29
  134.8 0.0 reduce-scatter.8.cloned.1.call-update
  134.9 52.2 %all-gather.2.cloned.1.call-done = bf16[2048,896]{1,0:T(8,128)(2,1)} async-done(((bf16[128,896]{1,0:T(8,128)(2,1)}), bf16[2048,896]{1,0:T(8,128)(2,1)}) %all-gather.2.cloned.1.call-update) | async-done | bytes 3670032 | tf_op jit(solution)/shard_map/all_gather | solution.py:37
  187.0 5.4 %fusion = f32[896,512]{1,0:T(8,128)} fusion(bf16[2048,896]{1,0:T(8,128)(2,1)} %all-gather.2.cloned.1.call-done, bf16[2048,512]{1,0:T(8,128)(2,1)S(1)} %bitcast.6), kind=kOutput, calls=%fused_computation.1 | convolution fusion | flops 1879048192 | bytes 7602176 | tf_op jit(solution)/shard_map/dot_general | solution.py:36
  192.4 0.0 reduce-scatter.8.cloned.1.call-done
Async XLA Ops:
  8.0 61.5 %copy-start = (bf16[896,512]{1,0:T(8,128)(2,1)S(1)}, bf16[896,512]{1,0:T(8,128)(2,1)}, u32[]{:S(2)}) copy-start(bf16[896,512]{1,0:T(8,128)(2,1)} %param.5) | copy-start | bytes 2752516
  8.0 87.4 %reduce-scatter.4.cloned.1.call-start = ((), (), s32[]{:S(2)}) async-start(), calls=%async_computation.4 | async-start | bytes 5505024 | tf_op jit(solution)/shard_map/reduce_scatter | solution.py:29
  73.7 61.2 %reduce-scatter.6.cloned.1.call-start = ((), (), s32[]{:S(2)}) async-start(), calls=%async_computation.5 | async-start | bytes 2293760 | tf_op jit(solution)/shard_map/reduce_scatter | solution.py:29
  95.4 91.6 %all-gather.2.cloned.1.call-start = ((), (), s32[]{:S(2)}) async-start(), calls=%async_computation.7 | async-start | bytes 3899392 | tf_op jit(solution)/shard_map/all_gather | solution.py:37
  96.0 96.4 %reduce-scatter.8.cloned.1.call-start = ((), (), s32[]{:S(2)}) async-start(), calls=%async_computation.6 | async-start | bytes 688128 | tf_op jit(solution)/shard_map/reduce_scatter | solution.py:29
Sparse Core Ops, SparseCore 0:
  73.8 21.5 reduce-scatter.3
  98.2 36.5 reduce-scatter.5
  138.2 44.1 reduce-scatter.7
Sparse Core Ops, SparseCore 1:
  99.2 87.8 all-gather.1
where the time goes:
time: 200 us
  waiting for transfers between devices  113 us (56%)
  blocking collectives  60.3 us (30%)
  between operations  15.2 us (8%)
  matrix products  9.52 us (5%)
    reduce_scatter x3, waiting for transfers between devices, own_rows(): running = lax.psum_scatter(running, axis, scatter_dimension=0, tiled=True)  60.5 us
    all_to_all x1, blocking collectives, sent_to_all(): return lax.all_to_all(copies, axis, split_axis=0, concat_axis=0, tiled=True)  60.3 us
    all_gather x1, waiting for transfers between devices, local(): lax.all_gather(hidden, DP_ROW, axis=0, tiled=True)  52.2 us
    dot_general x1, matrix products, local(): lax.dot_general(lax.all_gather(hidden, DP_ROW, axis=0, tiled=True), picke...  5.35 us
    dot_general x1, matrix products, local(): lax.dot_general(picked, weight, (((1,), (1,)), ((), ())), preferred_eleme...  4.17 us
  transfers between devices with their start and end apart: 4, of which 3 were waited for; matrix products, arithmetic and copies ran while one was open for 3% of the time, Pallas kernels for 0%

commit v1 on v0

v1 whole, which is shorter than its diff:
```python
import jax
import jax.numpy as jnp
from jax import lax
from jax.experimental import pallas as pl
from jax.experimental.pallas import tpu as pltpu
from jax.sharding import Mesh
from jax.sharding import PartitionSpec as P

DP_ROW = ("dp", "x", "zh")
COL = ("y", "zl")
MESH = pl.DeviceIdType.MESH
BF16 = jnp.bfloat16
F32 = jnp.float32


def rows(ref, start, count):
    return ref.at[pl.ds(pl.multiple_of(start, 64), count)]


def done(ref, sem):
    pltpu.make_async_copy(ref, ref, sem).wait()


def kernel(
    hid_in, up_in, w_in, ig_out, dw_out,
    U, UP, H, W, WP, T, c1p, c1m, c2p, c2m, zs, zr, own, igv, dwv,
    s_loc, s_a1, s_yp, s_ym, s_up, s_w, s_bz, s_bxp, s_bxm, s_bfp, s_bfm, s_hd,
    s_c1p, s_c1m, s_c2p, s_c2m, s_z,
    t_u, t_up, t_w, t_h, t_hd, t_c, t_out,
):
    c = lax.axis_index("dp")
    x = lax.axis_index("x")
    h = lax.axis_index("zh")
    y = lax.axis_index("y")
    l = lax.axis_index("zl")
    other = {"dp": 1 - c}
    xp = {"x": lax.rem(x + 1, 4)}
    xm = {"x": lax.rem(x + 3, 4)}
    yp = {"y": lax.rem(y + 1, 8)}
    ym = {"y": lax.rem(y + 7, 8)}
    zo = {"zh": 1 - h}
    line = [l, l + 1 - 2 * lax.rem(l, 2), lax.rem(l + 2, 4), 3 - l]
    mates = [{"zl": k} for k in line[1:]]

    def send(src, dst, t, s, to):
        pltpu.make_async_remote_copy(
            src_ref=src, dst_ref=dst, send_sem=t, recv_sem=s, device_id=to, device_id_type=MESH
        ).start()

    def urow(block, i):
        return (block * 4 + line[i]) * 64

    def hrow(core, xx, hh):
        return (core * 8 + xx * 2 + hh) * 128

    local_up = pltpu.make_async_copy(up_in, rows(U, urow(y, 0), 64), s_loc.at[0])
    local_hid = pltpu.make_async_copy(hid_in, rows(H, hrow(c, x, h), 128), s_loc.at[1])
    local_w = pltpu.make_async_copy(w_in, W, s_loc.at[2])
    local_up.start()
    local_hid.start()
    local_w.start()

    barrier = pltpu.get_barrier_semaphore()
    partners = mates + [yp, ym, xp, xm, zo, other]
    for to in partners:
        pl.semaphore_signal(barrier, inc=1, device_id=to, device_id_type=MESH)
    pl.semaphore_wait(barrier, len(partners))

    local_up.wait()
    mine = rows(U, urow(y, 0), 64)
    for i in range(1, 4):
        send(mine, mine, t_u, s_a1.at[i - 1], mates[i - 1])
    send(mine, mine, t_u, s_yp.at[0], yp)
    send(mine, mine, t_u, s_ym.at[0], ym)

    def to_partner(block, i):
        @pl.when(block // 4 != c)
        def _():
            b4 = lax.rem(block, 4)
            send(rows(U, urow(block, i), 64), rows(UP, (b4 * 4 + line[i]) * 64, 64), t_up, s_up.at[b4], other)

    to_partner(y, 0)

    local_hid.wait()

    def share(xx, hh, part, to, sem):
        piece = rows(H, hrow(c, xx, hh) + part * 64, 64)
        send(piece, piece, t_h, sem, to)

    share(x, h, 0, xp, s_bxp.at[0, 0])
    share(x, h, 1, xm, s_bxm.at[0, 1])
    share(x, h, 1, xp, s_bxp.at[0, 1])
    share(x, h, 0, xm, s_bxm.at[0, 0])

    def hid_across(xx, hh):
        piece = rows(H, hrow(c, xx, hh), 128)
        send(piece, piece, t_hd, s_hd.at[0], other)

    hid_across(x, h)
    local_w.wait()
    send(W, WP, t_w, s_w.at[0], other)

    for i in range(1, 4):
        piece = rows(U, urow(y, i), 64)
        done(piece, s_a1.at[i - 1])
        send(piece, piece, t_u, s_yp.at[i], yp)
        send(piece, piece, t_u, s_ym.at[i], ym)
        to_partner(y, i)
        if i == 1:
            share(x, h, 0, zo, s_bz.at[0])
            share(x, h, 1, zo, s_bz.at[1])
    done(WP, s_w.at[0])

    def quarter(xx, hh, ab):
        return T.at[xx, pl.ds(pl.multiple_of(hh * 128 + ab * 64, 64), 64)]

    sides = (1 - h, h)

    def block_step(delta):
        block = lax.rem(y + delta + 8, 8)
        b4 = lax.rem(block, 4)
        d = lax.rem(b4 - x + 4, 4)

        @pl.when(block // 4 == c)
        def _():
            done(rows(UP, b4 * 256, 256), s_up.at[b4])
            u = rows(U, block * 256, 256)
            up = rows(UP, b4 * 256, 256)
            dims = (((1,), (1,)), ((), ()))
            for n0 in range(0, 896, 256):
                n1 = min(n0 + 256, 896)
                acc = lax.dot_general(u[...], W[n0:n1], dims, preferred_element_type=F32)
                acc += lax.dot_general(up[...], WP[n0:n1], dims, preferred_element_type=F32)
                T[b4, :, n0:n1] = acc.astype(BF16)

            @pl.when(d == 2)
            def _():
                for k in range(2):
                    send(quarter(b4, sides[k], 0), c1p.at[k], t_c, s_c1p.at[k], xp)
                    send(quarter(b4, sides[k], 1), c1m.at[k], t_c, s_c1m.at[k], xm)

            @pl.when(d == 1)
            def _():
                for k in range(2):
                    send(quarter(b4, sides[k], 1), c2p.at[k, 1], t_c, s_c2p.at[k, 1], xp)

            @pl.when(d == 3)
            def _():
                for k in range(2):
                    send(quarter(b4, sides[k], 0), c2m.at[k, 0], t_c, s_c2m.at[k, 0], xm)

    def add_step(delta):
        block = lax.rem(y + delta + 8, 8)
        b4 = lax.rem(block, 4)
        d = lax.rem(b4 - x + 4, 4)
        here = block // 4 == c

        @pl.when(jnp.logical_and(here, d == 1))
        def _():
            for k in range(2):
                done(c1p.at[k], s_c1p.at[k])
                q = quarter(b4, sides[k], 0)
                q[...] = (q[...].astype(F32) + c1p[k].astype(F32)).astype(BF16)
                send(q, c2p.at[k, 0], t_c, s_c2p.at[k, 0], xp)

        @pl.when(jnp.logical_and(here, d == 3))
        def _():
            for k in range(2):
                done(c1m.at[k], s_c1m.at[k])
                q = quarter(b4, sides[k], 1)
                q[...] = (q[...].astype(F32) + c1m[k].astype(F32)).astype(BF16)
                send(q, c2m.at[k, 1], t_c, s_c2m.at[k, 1], xm)

    def sum_step(delta):
        block = lax.rem(y + delta + 8, 8)
        b4 = lax.rem(block, 4)
        d = lax.rem(b4 - x + 4, 4)

        @pl.when(jnp.logical_and(block // 4 == c, d == 0))
        def _():
            for k in range(2):
                for p in (1, 0):
                    done(c2p.at[k, p], s_c2p.at[k, p])
                    done(c2m.at[k, p], s_c2m.at[k, p])
                    total = quarter(b4, sides[k], p)[...].astype(F32) + c2p[k, p].astype(F32) + c2m[k, p].astype(F32)
                    if k == 0:
                        zs[p] = total.astype(BF16)
                        send(zs.at[p], zr.at[p], t_c, s_z.at[p], zo)
                    else:
                        own[p] = total

    block_step(0)

    def forward(e_x, hh, e):
        left, right = lax.rem(x + 3, 4), lax.rem(x + 1, 4)
        done(rows(H, hrow(c, left, hh), 64), s_bxp.at[e, 0])
        share(left, hh, 0, xp, s_bfp.at[e])
        done(rows(H, hrow(c, right, hh) + 64, 64), s_bxm.at[e, 1])
        share(right, hh, 1, xm, s_bfm.at[e])

    def across_near(hh, e):
        left, right = lax.rem(x + 3, 4), lax.rem(x + 1, 4)
        done(rows(H, hrow(c, left, hh) + 64, 64), s_bxp.at[e, 1])
        hid_across(left, hh)
        done(rows(H, hrow(c, right, hh), 64), s_bxm.at[e, 0])
        hid_across(right, hh)

    def across_far(hh, e):
        far = lax.rem(x + 2, 4)
        done(rows(H, hrow(c, far, hh), 64), s_bfp.at[e])
        done(rows(H, hrow(c, far, hh) + 64, 64), s_bfm.at[e])
        hid_across(far, hh)

    def from_z(part):
        done(rows(H, hrow(c, x, 1 - h) + part * 64, 64), s_bz.at[part])
        first, second = (xp, xm) if part == 0 else (xm, xp)
        share(x, 1 - h, part, xp, s_bxp.at[1, part])
        share(x, 1 - h, part, xm, s_bxm.at[1, part])
        if part == 1:
            hid_across(x, 1 - h)

    tasks = {
        (1, 0): [lambda: forward(x, h, 0)],
        (1, 2): [lambda: from_z(0), lambda: add_step(0)],
        (2, 0): [lambda: from_z(1), lambda: sum_step(0)],
        (2, 1): [lambda: across_near(h, 0)],
        (2, 2): [lambda: add_step(1), lambda: add_step(-1)],
        (2, 3): [lambda: across_far(h, 0)],
        (3, 0): [lambda: sum_step(1), lambda: sum_step(-1)],
        (3, 1): [lambda: forward(x, 1 - h, 1)],
        (3, 2): [lambda: add_step(2), lambda: add_step(-2), lambda: across_near(1 - h, 1)],
        (4, 0): [lambda: sum_step(2), lambda: sum_step(-2)],
        (4, 1): [],
    }
    for stage in range(1, 5):
        plus = lax.rem(y - stage + 8, 8)
        minus = lax.rem(y + stage, 8)
        for i in range(4 if stage < 4 else 2):
            n = (stage - 1) * 4 + i
            ip, im = (i, i) if stage < 4 else (i, i + 2)
            piece = rows(U, urow(plus, ip), 64)
            done(piece, s_yp.at[n])
            if n < 10:
                send(piece, piece, t_u, s_yp.at[n + 4], yp)
            to_partner(plus, ip)
            piece = rows(U, urow(minus, im), 64)
            done(piece, s_ym.at[n])
            if n < 8:
                send(piece, piece, t_u, s_ym.at[n + 4], ym)
            elif n in (10, 11):
                send(piece, piece, t_u, s_ym.at[n + 2], ym)
            to_partner(minus, im)
            for task in tasks.get((stage, i), []):
                task()
        if stage < 4:
            block_step(-stage)
            block_step(stage)
        else:
            block_step(4)

    across_far(1 - h, 1)
    add_step(3)
    add_step(-3)
    done(rows(H, (1 - c) * 1024, 1024), s_hd.at[0])

    def dw_tile(f):
        cols = slice(f * 128, f * 128 + 128)
        dwv[cols] = lax.dot_general(H[:, cols], U[...], (((0,), (0,)), ((), ())), preferred_element_type=F32)
        pltpu.make_async_copy(dwv.at[cols], dw_out.at[cols], t_out).start()

    dw_tile(0)
    add_step(4)
    dw_tile(1)
    sum_step(3)
    sum_step(-3)
    dw_tile(2)
    dw_tile(3)
    sum_step(4)
    dw_tile(4)
    dw_tile(5)
    dw_tile(6)
    for p in range(2):
        done(zr.at[p], s_z.at[p])
        igv[p] = (own[p] + zr[p].astype(F32)).astype(BF16)
        pltpu.make_async_copy(igv.at[p], ig_out.at[p * 64 : p * 64 + 64], s_loc.at[p]).start()

    done(rows(U, 0, 1984), t_u)
    done(UP, t_up)
    done(W, t_w)
    done(rows(H, 0, 1024), t_hd)
    done(rows(H, 0, 896), t_h)
    done(rows(H, 0, 896), t_c)
    done(dwv, t_out)
    done(igv.at[0], s_loc.at[0])
    done(igv.at[1], s_loc.at[1])


def local(hidden, upstream, weight):
    dma = pltpu.SemaphoreType.DMA
    return pl.pallas_call(
        kernel,
        out_shape=(jax.ShapeDtypeStruct((128, 896), BF16), jax.ShapeDtypeStruct((896, 512), F32)),
        in_specs=[pl.BlockSpec(memory_space=pl.ANY)] * 3,
        out_specs=[pl.BlockSpec(memory_space=pl.ANY)] * 2,
        scratch_shapes=[
            pltpu.VMEM((2048, 512), BF16),
            pltpu.VMEM((1024, 512), BF16),
            pltpu.VMEM((2048, 896), BF16),
            pltpu.VMEM((896, 512), BF16),
            pltpu.VMEM((896, 512), BF16),
            pltpu.VMEM((4, 256, 896), BF16),
            pltpu.VMEM((2, 64, 896), BF16),
            pltpu.VMEM((2, 64, 896), BF16),
            pltpu.VMEM((2, 2, 64, 896), BF16),
            pltpu.VMEM((2, 2, 64, 896), BF16),
            pltpu.VMEM((2, 64, 896), BF16),
            pltpu.VMEM((2, 64, 896), BF16),
            pltpu.VMEM((2, 64, 896), F32),
            pltpu.VMEM((2, 64, 896), BF16),
            pltpu.VMEM((896, 512), F32),
            dma((3,)), dma((3,)), dma((14,)), dma((14,)), dma((4,)), dma((1,)), dma((2,)),
            dma((2, 2)), dma((2, 2)), dma((2,)), dma((2,)), dma((1,)),
            dma((2,)), dma((2,)), dma((2, 2)), dma((2, 2)), dma((2,)),
            dma, dma, dma, dma, dma, dma, dma,
        ],
        compiler_params=pltpu.CompilerParams(
            collective_id=0, has_side_effects=True, vmem_limit_bytes=48 << 20
        ),
    )(hidden, upstream, weight)


def solution(mesh):
    finer = Mesh(mesh.devices.reshape(2, 4, 2, 8, 4), ("dp", "x", "zh", "y", "zl"))
    placed = (P(DP_ROW, COL), P(COL, DP_ROW), P(COL, DP_ROW))
    return jax.shard_map(
        local,
        mesh=finer,
        in_specs=placed,
        out_specs=(P(DP_ROW, COL), P(COL, DP_ROW)),
        check_vma=False,
    )
```

time: 200 us -> 80.2 us (0.40)
  the two profiles are of different devices: /device:TPU:129 before, /device:TPU:106 now
where the time goes in v1:
time: 80.2 us; the launch traced here: 80 us
  Pallas kernels  74.5 us (93%)
  local copies, waits for them, and re-layouts  4.87 us (6%)
    pallas_call x1, Pallas kernels, local(): pl.pallas_call(kernel, out_shape=(jax.ShapeDtypeStruct((128, 896), BF16),...  74.5 us
    unnamed x8, local copies, waits for them, and re-layouts  4.87 us

profile of v1, /device:TPU:106, one launch (start us, length us, event | category | flops | bytes accessed | tf_op | source)
XLA Modules:
  0.0 80.0 jit_solution(11148224513130709368)
XLA Ops:
  0.6 0.0 copy-start
  0.6 1.2 %copy-done = bf16[896,512]{1,0:T(8,128)(2,1)S(1)} copy-done((bf16[896,512]{1,0:T(8,128)(2,1)S(1)}, bf16[896,512]{1,0:T(8,128)(2,1)}, u32[]{:S(2)}) %copy-start) | copy-done | bytes 917528
  1.8 0.0 copy-start.1
  1.8 0.9 %copy-done.1 = bf16[128,896]{1,0:T(8,128)(2,1)S(1)} copy-done((bf16[128,896]{1,0:T(8,128)(2,1)S(1)}, bf16[128,896]{1,0:T(8,128)(2,1)}, u32[]{:S(2)}) %copy-start.1) | copy-done | bytes 229400
  2.7 0.0 copy-start.2
  2.8 0.8 %copy-done.2 = bf16[64,512]{1,0:T(8,128)(2,1)S(1)} copy-done((bf16[64,512]{1,0:T(8,128)(2,1)S(1)}, bf16[64,512]{1,0:T(8,128)(2,1)}, u32[]{:S(2)}) %copy-start.2) | copy-done | bytes 65560
  3.6 74.5 %shard_map.50 = (bf16[128,896]{1,0:T(8,128)(2,1)S(1)}, f32[896,512]{1,0:T(8,128)S(1)}) custom-call(bf16[128,896]{1,0:T(8,128)(2,1)S(1)} %copy-done.1, bf16[64,512]{1,0:T(8,128)(2,1)S(1)} %copy-done.2, bf16[896,512]{1,0:T(8,128)(2,1)S(1)} %copy-done), custom_call_target="tpu_custom_call" | custom-call | tf_op jit(solution)/shard_map/pallas_call | solution.py:300
  78.1 0.7 copy.7
  78.7 1.2 %copy.8 = f32[896,512]{1,0:T(8,128)} copy(f32[896,512]{1,0:T(8,128)S(1)} %get-tuple-element.5) | data formatting | bytes 3670016
Async XLA Ops:
  0.6 1.2 %copy-start = (bf16[896,512]{1,0:T(8,128)(2,1)S(1)}, bf16[896,512]{1,0:T(8,128)(2,1)}, u32[]{:S(2)}) copy-start(bf16[896,512]{1,0:T(8,128)(2,1)} %w_in.1) | copy-start | bytes 2752516
  1.8 0.9 %copy-start.1 = (bf16[128,896]{1,0:T(8,128)(2,1)S(1)}, bf16[128,896]{1,0:T(8,128)(2,1)}, u32[]{:S(2)}) copy-start(bf16[128,896]{1,0:T(8,128)(2,1)} %hid_in.1) | copy-start | bytes 688132
  2.7 0.8 %copy-start.2 = (bf16[64,512]{1,0:T(8,128)(2,1)S(1)}, bf16[64,512]{1,0:T(8,128)(2,1)}, u32[]{:S(2)}) copy-start(bf16[64,512]{1,0:T(8,128)(2,1)} %up_in.1) | copy-start | bytes 196612

commit v2 on v1

v2 whole, which is shorter than its diff:
```python
import jax
import jax.numpy as jnp
from jax import lax
from jax.experimental import pallas as pl
from jax.experimental.pallas import tpu as pltpu
from jax.sharding import Mesh
from jax.sharding import PartitionSpec as P

DP_ROW = ("dp", "x", "zh")
COL = ("y", "zl")
MESH = pl.DeviceIdType.MESH
BF16 = jnp.bfloat16
F32 = jnp.float32


def rows(ref, start, count):
    return ref.at[pl.ds(pl.multiple_of(start, 64), count)]


def done(ref, sem):
    pltpu.make_async_copy(ref, ref, sem).wait()


STEPS = (
    "01", "10", "02", "11", "03", "bz:0", "wp:0", "fwd:0",
    "20", "T:0", "bz:1", "12", "13", "21", "T:1", "T:-1",
    "far:0", "fz:0", "fz:1", "22", "near:0", "23", "add:0", "adb:0",
    "30", "T:2", "T:-2", "31", "add:1", "add:-1", "adb:1", "adb:-1",
    "32", "sum:0", "33", "40", "T:-3", "T:3", "41", "42",
    "add:-2", "add:2", "adb:-2", "adb:2", "43",
)
TAIL = (
    "T:4", "z:0", "z:1", "sum:1", "sum:-1", "sum:-2", "sum:2", "add:-3",
    "add:3", "adb:-3", "adb:3", "add:4", "adb:4", "near:1", "far:1", "hd:0",
    "dw:0", "sum:-3", "sum:3", "dw:1", "sum:4", "own:0", "own:1", "own:-1",
    "own:2", "own:-2", "own:-3", "own:3", "own:4", "dw:2", "dw:3", "dw:4",
    "dw:5", "dw:6",
)


def kernel(
    hid_in, up_in, w_in, ig_out, dw_out,
    U, UP, H, W, WP, T, c1p, c1m, c2p, c2m, zs, zr, own,
    s_loc, s_a1, s_yp, s_ym, s_up, s_w, s_bz, s_bxp, s_bxm, s_bf, s_bfz, s_hd,
    s_c1p, s_c1m, s_c2p, s_c2m, s_z,
    t_u, t_up, t_w, t_h, t_hd, t_c,
):
    c = lax.axis_index("dp")
    x = lax.axis_index("x")
    h = lax.axis_index("zh")
    y = lax.axis_index("y")
    l = lax.axis_index("zl")
    other = {"dp": 1 - c}
    xp = {"x": lax.rem(x + 1, 4)}
    xm = {"x": lax.rem(x + 3, 4)}
    yp = {"y": lax.rem(y + 1, 8)}
    ym = {"y": lax.rem(y + 7, 8)}
    zo = {"zh": 1 - h}
    line = [l, l + 1 - 2 * lax.rem(l, 2), lax.rem(l + 2, 4), 3 - l]
    mates = [{"zl": k} for k in line[1:]]

    def send(src, dst, t, s, to):
        pltpu.make_async_remote_copy(
            src_ref=src, dst_ref=dst, send_sem=t, recv_sem=s, device_id=to, device_id_type=MESH
        ).start()

    def urow(block, i):
        return (block * 4 + line[i]) * 64

    def hrow(core, xx, hh):
        return (core * 8 + xx * 2 + hh) * 128

    local_up = pltpu.make_async_copy(up_in, rows(U, urow(y, 0), 64), s_loc.at[0])
    local_hid = pltpu.make_async_copy(hid_in, rows(H, hrow(c, x, h), 128), s_loc.at[1])
    local_w = pltpu.make_async_copy(w_in, W, s_loc.at[2])
    local_up.start()
    local_hid.start()
    local_w.start()

    barrier = pltpu.get_barrier_semaphore()
    partners = mates + [yp, ym, xp, xm, zo, other]
    for to in partners:
        pl.semaphore_signal(barrier, inc=1, device_id=to, device_id_type=MESH)
    with jax.named_scope('barrier'):
        pl.semaphore_wait(barrier, len(partners))

    with jax.named_scope('lup'):
        local_up.wait()
    mine = rows(U, urow(y, 0), 64)
    for i in range(1, 4):
        send(mine, mine, t_u, s_a1.at[i - 1], mates[i - 1])

    def to_partner(block, i):
        @pl.when(block // 4 != c)
        def _():
            b4 = lax.rem(block, 4)
            send(rows(U, urow(block, i), 64), rows(UP, (b4 * 4 + line[i]) * 64, 64), t_up, s_up.at[b4], other)

    to_partner(y, 0)
    send(mine, mine, t_u, s_yp.at[0], yp)
    send(mine, mine, t_u, s_ym.at[0], ym)

    with jax.named_scope('lhid'):
        local_hid.wait()

    def share(xx, hh, part, to, sem):
        piece = rows(H, hrow(c, xx, hh) + part * 64, 64)
        send(piece, piece, t_h, sem, to)

    share(x, h, 0, xp, s_bxp.at[0, 0])
    share(x, h, 1, xm, s_bxm.at[0, 1])
    share(x, h, 1, xp, s_bxp.at[0, 1])
    share(x, h, 0, xm, s_bxm.at[0, 0])

    def hid_across(xx, hh):
        piece = rows(H, hrow(c, xx, hh), 128)
        send(piece, piece, t_hd, s_hd.at[0], other)

    hid_across(x, h)
    with jax.named_scope('lw'):
        local_w.wait()
    send(W, WP, t_w, s_w.at[0], other)

    wp = rows(WP, 0, 896)

    def quarter(xx, hh, ab):
        return T.at[xx, pl.ds(pl.multiple_of(hh * 128 + ab * 64, 64), 64)]

    sides = (1 - h, h)

    def place_of(delta):
        block = lax.rem(y + delta + 8, 8)
        b4 = lax.rem(block, 4)
        return block, b4, block // 4 == c, lax.rem(b4 - x + 4, 4)

    def spread(delta):
        _, b4, here, d = place_of(delta)

        @pl.when(jnp.logical_and(here, d == 2))
        def _():
            for k in range(2):
                send(quarter(b4, sides[k], 0), c1p.at[k], t_c, s_c1p.at[k], xp)
                send(quarter(b4, sides[k], 1), c1m.at[k], t_c, s_c1m.at[k], xm)

        @pl.when(jnp.logical_and(here, d == 1))
        def _():
            for k in range(2):
                send(quarter(b4, sides[k], 1), c2p.at[k, 1], t_c, s_c2p.at[k, 1], xp)

        @pl.when(jnp.logical_and(here, d == 3))
        def _():
            for k in range(2):
                send(quarter(b4, sides[k], 0), c2m.at[k, 0], t_c, s_c2m.at[k, 0], xm)

    def block_step(delta):
        block, b4, here, d = place_of(delta)

        @pl.when(here)
        def _():
            done(rows(UP, b4 * 256, 256), s_up.at[b4])
            u = rows(U, block * 256, 256)
            up = rows(UP, b4 * 256, 256)
            dims = (((1,), (1,)), ((), ()))
            for n0 in range(0, 896, 256):
                n1 = min(n0 + 256, 896)
                acc = lax.dot_general(u[...], W[n0:n1], dims, preferred_element_type=F32)
                acc += lax.dot_general(up[...], WP[n0:n1], dims, preferred_element_type=F32)
                T[b4, :, n0:n1] = acc.astype(BF16)

        spread(delta)

    def add_step(delta, k):
        _, b4, here, d = place_of(delta)

        @pl.when(jnp.logical_and(here, d == 1))
        def _():
            done(c1p.at[k], s_c1p.at[k])
            q = quarter(b4, sides[k], 0)
            q[...] = (q[...].astype(F32) + c1p[k].astype(F32)).astype(BF16)
            send(q, c2p.at[k, 0], t_c, s_c2p.at[k, 0], xp)

        @pl.when(jnp.logical_and(here, d == 3))
        def _():
            done(c1m.at[k], s_c1m.at[k])
            q = quarter(b4, sides[k], 1)
            q[...] = (q[...].astype(F32) + c1m[k].astype(F32)).astype(BF16)
            send(q, c2m.at[k, 1], t_c, s_c2m.at[k, 1], xm)

    def sum_step(delta, k):
        _, b4, here, d = place_of(delta)

        @pl.when(jnp.logical_and(here, d == 0))
        def _():
            for p in (1, 0):
                done(c2p.at[k, p], s_c2p.at[k, p])
                done(c2m.at[k, p], s_c2m.at[k, p])
                total = quarter(b4, sides[k], p)[...].astype(F32) + c2p[k, p].astype(F32) + c2m[k, p].astype(F32)
                if k == 0:
                    zs[p] = total.astype(BF16)
                    send(zs.at[p], zr.at[p], t_c, s_z.at[p], zo)
                else:
                    own[p] = total

    def last_step():
        for p in range(2):
            done(zr.at[p], s_z.at[p])
            ig_out[p * 64 : p * 64 + 64] = (own[p] + zr[p].astype(F32)).astype(BF16)

    def forward(hh, e):
        left, right = lax.rem(x + 3, 4), lax.rem(x + 1, 4)
        done(rows(H, hrow(c, left, hh), 64), s_bxp.at[e, 0])
        share(left, hh, 0, xp, s_bf.at[0])
        done(rows(H, hrow(c, right, hh) + 64, 64), s_bxm.at[e, 1])
        share(right, hh, 1, xm, s_bf.at[1])

    def across_near(hh, e):
        left, right = lax.rem(x + 3, 4), lax.rem(x + 1, 4)
        for part in (0, 1) if e == 1 else (1,):
            done(rows(H, hrow(c, left, hh) + part * 64, 64), s_bxp.at[e, part])
        hid_across(left, hh)
        for part in (1, 0) if e == 1 else (0,):
            done(rows(H, hrow(c, right, hh) + part * 64, 64), s_bxm.at[e, part])
        hid_across(right, hh)

    def across_far(hh, e):
        far = lax.rem(x + 2, 4)
        s_a, s_b = (s_bf.at[0], s_bf.at[1]) if e == 0 else (s_bfz.at[0], s_bfz.at[1])
        done(rows(H, hrow(c, far, hh), 64), s_a)
        done(rows(H, hrow(c, far, hh) + 64, 64), s_b)
        hid_across(far, hh)

    def far_along_z(part):
        share(lax.rem(x + 2, 4), h, part, zo, s_bfz.at[part])

    def from_z(part):
        done(rows(H, hrow(c, x, 1 - h) + part * 64, 64), s_bz.at[part])
        first, second = (xp, xm) if part == 0 else (xm, xp)
        share(x, 1 - h, part, xp, s_bxp.at[1, part])
        share(x, 1 - h, part, xm, s_bxm.at[1, part])
        if part == 1:
            hid_across(x, 1 - h)

    def halves():
        done(rows(H, (1 - c) * 1024, 1024), s_hd.at[0])

    def dw_tile(f):
        cols = slice(f * 128, f * 128 + 128)
        dw_out[cols] = lax.dot_general(H[:, cols], U[...], (((0,), (0,)), ((), ())), preferred_element_type=F32)

    ways = {
        "T": block_step,
        "add": lambda delta: add_step(delta, 0),
        "adb": lambda delta: add_step(delta, 1),
        "sum": lambda delta: sum_step(delta, 0),
        "own": lambda delta: sum_step(delta, 1),
        "dw": dw_tile,
        "z": from_z,
        "bz": lambda p: share(x, h, p, zo, s_bz.at[p]),
        "fwd": lambda _: forward(h, 0),
        "fz": far_along_z,
        "near": lambda e: across_near((h, 1 - h)[e], e),
        "far": lambda e: across_far((h, 1 - h)[e], e),
        "hd": lambda _: halves(),
        "wp": lambda _: done(wp, s_w.at[0]),
    }

    def run(line_of_tasks):
        for task in line_of_tasks:
            name, number = task.split(":")
            with jax.named_scope(task.replace(":", "_").replace("-", "m")):
                ways[name](int(number))

    def onward(k, i):
        if k == 0:
            piece = rows(U, urow(y, i), 64)
            with jax.named_scope(f"a1_{i}"):
                done(piece, s_a1.at[i - 1])
            send(piece, piece, t_u, s_yp.at[i], yp)
            send(piece, piece, t_u, s_ym.at[i], ym)
            to_partner(y, i)
            return
        n = k * 4 + i
        for block, sem, to, last in (
            (lax.rem(y - k + 8, 8), s_yp, yp, (0, 1)),
            (lax.rem(y + k, 8), s_ym, ym, (2, 3)),
        ):
            if k == 4 and i not in last:
                continue
            piece = rows(U, urow(block, i), 64)
            with jax.named_scope(f"y{k}_{i}"):
                done(piece, sem.at[n - 4])
            if k < 3 or (k == 3 and i in last):
                send(piece, piece, t_u, sem.at[n], to)
            to_partner(block, i)

    for step in STEPS:
        if ":" in step:
            run((step,))
        else:
            onward(int(step[0]), int(step[1]))
    run(TAIL)
    with jax.named_scope('last'):
        last_step()

    with jax.named_scope('fin'):
        done(rows(U, 0, 1984), t_u)
    done(UP, t_up)
    done(W, t_w)
    done(rows(H, 0, 1024), t_hd)
    done(rows(H, 0, 896), t_h)
    done(rows(H, 0, 896), t_c)


def local(hidden, upstream, weight):
    dma = pltpu.SemaphoreType.DMA
    hidden, upstream, weight = (pltpu.with_memory_space_constraint(a, pltpu.HBM) for a in (hidden, upstream, weight))
    return pl.pallas_call(
        kernel,
        out_shape=(jax.ShapeDtypeStruct((128, 896), BF16), jax.ShapeDtypeStruct((896, 512), F32)),
        in_specs=[pl.BlockSpec(memory_space=pltpu.HBM)] * 3,
        out_specs=[pl.BlockSpec(memory_space=pltpu.VMEM)] * 2,
        scratch_shapes=[
            pltpu.VMEM((2048, 512), BF16),
            pltpu.VMEM((1024, 512), BF16),
            pltpu.VMEM((2048, 896), BF16),
            pltpu.VMEM((896, 512), BF16),
            pltpu.VMEM((896, 512), BF16),
            pltpu.VMEM((4, 256, 896), BF16),
            pltpu.VMEM((2, 64, 896), BF16),
            pltpu.VMEM((2, 64, 896), BF16),
            pltpu.VMEM((2, 2, 64, 896), BF16),
            pltpu.VMEM((2, 2, 64, 896), BF16),
            pltpu.VMEM((2, 64, 896), BF16),
            pltpu.VMEM((2, 64, 896), BF16),
            pltpu.VMEM((2, 64, 896), F32),
            dma((3,)), dma((3,)), dma((16,)), dma((16,)), dma((4,)), dma((1,)), dma((2,)),
            dma((2, 2)), dma((2, 2)), dma((2,)), dma((2,)), dma((1,)),
            dma((2,)), dma((2,)), dma((2, 2)), dma((2, 2)), dma((2,)),
            dma, dma, dma, dma, dma, dma,
        ],
        compiler_params=pltpu.CompilerParams(
            collective_id=0, has_side_effects=True, vmem_limit_bytes=40 << 20
        ),
    )(hidden, upstream, weight)


def solution(mesh):
    finer = Mesh(mesh.devices.reshape(2, 4, 2, 8, 4), ("dp", "x", "zh", "y", "zl"))
    placed = (P(DP_ROW, COL), P(COL, DP_ROW), P(COL, DP_ROW))
    return jax.shard_map(
        local,
        mesh=finer,
        in_specs=placed,
        out_specs=(P(DP_ROW, COL), P(COL, DP_ROW)),
        check_vma=False,
    )
```

time: 80.2 us -> 61.7 us (0.77)
  the two profiles are of different devices: /device:TPU:106 before, /device:TPU:24 now
where the time goes in v2:
time: 61.7 us; the launch traced here: 61.6 us
  Pallas kernels  59 us (96%)
  local copies, waits for them, and re-layouts  1.92 us (3%)
  between operations  0.64 us (1%)
    pallas_call x1, Pallas kernels, local(): pl.pallas_call(kernel, out_shape=(jax.ShapeDtypeStruct((128, 896), BF16),...  59 us
    unnamed x2, local copies, waits for them, and re-layouts  1.92 us

profile of v2, /device:TPU:24, one launch (start us, length us, event | category | flops | bytes accessed | tf_op | source)
XLA Modules:
  0.0 61.6 jit_solution(14517041474864074163)
XLA Ops:
  0.6 59.0 %shard_map.50 = (bf16[128,896]{1,0:T(8,128)(2,1)S(1)}, f32[896,512]{1,0:T(8,128)S(1)}) custom-call(bf16[128,896]{1,0:T(8,128)(2,1)} %hid_in.1, bf16[64,512]{1,0:T(8,128)(2,1)} %up_in.1, bf16[896,512]{1,0:T(8,128)(2,1)} %w_in.1), custom_call_target="tpu_custom_call" | custom-call | tf_op jit(solution)/shard_map/pallas_call | solution.py:317
  59.7 0.7 %copy.7 = bf16[128,896]{1,0:T(8,128)(2,1)} copy(bf16[128,896]{1,0:T(8,128)(2,1)S(1)} %get-tuple-element.4) | data formatting | bytes 458752
  60.4 1.2 %copy.8 = f32[896,512]{1,0:T(8,128)} copy(f32[896,512]{1,0:T(8,128)S(1)} %get-tuple-element.5) | data formatting | bytes 3670016

commit v3 on v2

--- a/solution.py
+++ b/solution.py
@@ -22,19 +22,19 @@
 
 
 STEPS = (
-    "01", "10", "02", "11", "03", "bz:0", "wp:0", "fwd:0",
-    "20", "T:0", "bz:1", "12", "13", "21", "T:1", "T:-1",
+    "10", "01", "02", "20", "03", "bz:0", "wp:0", "fwd:0",
+    "11", "T:0", "bz:1", "12", "13", "21", "T:1", "T:-1",
     "far:0", "fz:0", "fz:1", "22", "near:0", "23", "add:0", "adb:0",
     "30", "T:2", "T:-2", "31", "add:1", "add:-1", "adb:1", "adb:-1",
     "32", "sum:0", "33", "40", "T:-3", "T:3", "41", "42",
-    "add:-2", "add:2", "adb:-2", "adb:2", "43",
+    "add:-2", "add:2", "adb:-2", "adb:2", "43", "T:4",
 )
 TAIL = (
-    "T:4", "z:0", "z:1", "sum:1", "sum:-1", "sum:-2", "sum:2", "add:-3",
-    "add:3", "adb:-3", "adb:3", "add:4", "adb:4", "near:1", "far:1", "hd:0",
-    "dw:0", "sum:-3", "sum:3", "dw:1", "sum:4", "own:0", "own:1", "own:-1",
-    "own:2", "own:-2", "own:-3", "own:3", "own:4", "dw:2", "dw:3", "dw:4",
-    "dw:5", "dw:6",
+    "z:0", "z:1", "sum:1", "sum:-1", "add:-3", "add:3", "adb:-3", "adb:3",
+    "sum:-2", "sum:2", "add:4", "adb:4", "sum:-3", "sum:3", "near:1", "sum:4",
+    "far:1", "hd:0", "dw:0", "dw:1", "dw:2", "own:0", "own:1", "own:-1",
+    "own:2", "own:-2", "own:-3", "own:3", "own:4", "dw:3", "dw:4", "dw:5",
+    "dw:6",
 )
 
 

time: 61.7 us -> 60.3 us (0.977)
  the two profiles are of different devices: /device:TPU:24 before, /device:TPU:1 now
where the time goes in v3:
time: 60.3 us; the launch traced here: 60.2 us
  Pallas kernels  57.6 us (96%)
  local copies, waits for them, and re-layouts  1.92 us (3%)
  between operations  0.64 us (1%)
    pallas_call x1, Pallas kernels, local(): pl.pallas_call(kernel, out_shape=(jax.ShapeDtypeStruct((128, 896), BF16),...  57.6 us
    unnamed x2, local copies, waits for them, and re-layouts  1.92 us

profile of v3, /device:TPU:1, one launch (start us, length us, event | category | flops | bytes accessed | tf_op | source)
XLA Modules:
  0.0 60.2 jit_solution(3909075545741488580)
XLA Ops:
  0.6 57.6 %shard_map.50 = (bf16[128,896]{1,0:T(8,128)(2,1)S(1)}, f32[896,512]{1,0:T(8,128)S(1)}) custom-call(bf16[128,896]{1,0:T(8,128)(2,1)} %hid_in.1, bf16[64,512]{1,0:T(8,128)(2,1)} %up_in.1, bf16[896,512]{1,0:T(8,128)(2,1)} %w_in.1), custom_call_target="tpu_custom_call" | custom-call | tf_op jit(solution)/shard_map/pallas_call | solution.py:317
  58.2 0.7 %copy.7 = bf16[128,896]{1,0:T(8,128)(2,1)} copy(bf16[128,896]{1,0:T(8,128)(2,1)S(1)} %get-tuple-element.4) | data formatting | bytes 458752
  58.9 1.2 %copy.8 = f32[896,512]{1,0:T(8,128)} copy(f32[896,512]{1,0:T(8,128)S(1)} %get-tuple-element.5) | data formatting | bytes 3670016

commit v4 on v3

--- a/solution.py
+++ b/solution.py
@@ -311,10 +311,21 @@
     done(rows(H, 0, 896), t_c)
 
 
+def put_out(grad, weight_grad, grad_out, weight_grad_out, sems):
+    copies = [pltpu.make_async_copy(grad, grad_out, sems.at[7])]
+    for f in range(7):
+        part = pl.ds(f * 128, 128)
+        copies.append(pltpu.make_async_copy(weight_grad.at[part], weight_grad_out.at[part], sems.at[f]))
+    for copy in copies:
+        copy.start()
+    for copy in copies:
+        copy.wait()
+
+
 def local(hidden, upstream, weight):
     dma = pltpu.SemaphoreType.DMA
     hidden, upstream, weight = (pltpu.with_memory_space_constraint(a, pltpu.HBM) for a in (hidden, upstream, weight))
-    return pl.pallas_call(
+    grad, weight_grad = pl.pallas_call(
         kernel,
         out_shape=(jax.ShapeDtypeStruct((128, 896), BF16), jax.ShapeDtypeStruct((896, 512), F32)),
         in_specs=[pl.BlockSpec(memory_space=pltpu.HBM)] * 3,
@@ -342,6 +353,14 @@
             collective_id=0, has_side_effects=True, vmem_limit_bytes=40 << 20
         ),
     )(hidden, upstream, weight)
+    return pl.pallas_call(
+        put_out,
+        out_shape=(pltpu.HBM((128, 896), BF16), pltpu.HBM((896, 512), F32)),
+        in_specs=[pl.BlockSpec(memory_space=pltpu.VMEM)] * 2,
+        out_specs=[pl.BlockSpec(memory_space=pltpu.HBM)] * 2,
+        scratch_shapes=[dma((8,))],
+        compiler_params=pltpu.CompilerParams(vmem_limit_bytes=8 << 20),
+    )(*(pltpu.with_memory_space_constraint(a, pltpu.VMEM) for a in (grad, weight_grad)))
 
 
 def solution(mesh):

time: 60.3 us -> 59.7 us (0.990)
  local copies, waits for them, and re-layouts: 1.92 us -> 0 us
  Pallas kernels: 57.6 us -> 59 us
    unnamed x2 -> x0, local copies, waits for them, and re-layouts: 1.92 us -> none
    pallas_call x0 -> x1, Pallas kernels: none -> 1.37 us  [local(): pl.pallas_call(put_out, out_shape=(pltpu.HBM((128, 896), BF16), pltpu.HBM...]
where the time goes in v4:
time: 59.7 us; the launch traced here: 59.6 us
  Pallas kernels  59 us (99%)
  between operations  0.64 us (1%)
    pallas_call x1, Pallas kernels, local(): pl.pallas_call(kernel, out_shape=(jax.ShapeDtypeStruct((128, 896), BF16),...  57.6 us
    pallas_call x1, Pallas kernels, local(): pl.pallas_call(put_out, out_shape=(pltpu.HBM((128, 896), BF16), pltpu.HBM...  1.37 us

profile of v4, /device:TPU:1, one launch (start us, length us, event | category | flops | bytes accessed | tf_op | source)
XLA Modules:
  0.0 59.6 jit_solution(8880639186210046870)
XLA Ops:
  0.6 57.6 %shard_map.50 = (bf16[128,896]{1,0:T(8,128)(2,1)S(1)}, f32[896,512]{1,0:T(8,128)S(1)}) custom-call(bf16[128,896]{1,0:T(8,128)(2,1)} %hid_in.1, bf16[64,512]{1,0:T(8,128)(2,1)} %up_in.1, bf16[896,512]{1,0:T(8,128)(2,1)} %w_in.1), custom_call_target="tpu_custom_call" | custom-call | tf_op jit(solution)/shard_map/pallas_call | solution.py:328
  58.2 1.4 %shard_map.51 = (bf16[128,896]{1,0:T(8,128)(2,1)}, f32[896,512]{1,0:T(8,128)}) custom-call(bf16[128,896]{1,0:T(8,128)(2,1)S(1)} %get-tuple-element.4.grad, f32[896,512]{1,0:T(8,128)S(1)} %get-tuple-element.5.weight_grad), custom_call_target="tpu_custom_call" | custom-call | tf_op jit(solution)/shard_map/pallas_call | solution.py:356

commit v5 on v4

--- a/solution.py
+++ b/solution.py
@@ -26,7 +26,7 @@
     "11", "T:0", "bz:1", "12", "13", "21", "T:1", "T:-1",
     "far:0", "fz:0", "fz:1", "22", "near:0", "23", "add:0", "adb:0",
     "30", "T:2", "T:-2", "31", "add:1", "add:-1", "adb:1", "adb:-1",
-    "32", "sum:0", "33", "40", "T:-3", "T:3", "41", "42",
+    "32", "sum:0", "33", "T:-3", "T:3", "40", "41", "42",
     "add:-2", "add:2", "adb:-2", "adb:2", "43", "T:4",
 )
 TAIL = (

time: 59.7 us -> 59.7 us (level)
  no operation moved by 1% of the time
where the time goes in v5:
time: 59.7 us; the launch traced here: 59.6 us
  Pallas kernels  59 us (99%)
  between operations  0.64 us (1%)
    pallas_call x1, Pallas kernels, local(): pl.pallas_call(kernel, out_shape=(jax.ShapeDtypeStruct((128, 896), BF16),...  57.6 us
    pallas_call x1, Pallas kernels, local(): pl.pallas_call(put_out, out_shape=(pltpu.HBM((128, 896), BF16), pltpu.HBM...  1.37 us

profile of v5, /device:TPU:1, one launch (start us, length us, event | category | flops | bytes accessed | tf_op | source)
XLA Modules:
  0.0 59.6 jit_solution(8391225690820814680)
XLA Ops:
  0.6 57.6 %shard_map.50 = (bf16[128,896]{1,0:T(8,128)(2,1)S(1)}, f32[896,512]{1,0:T(8,128)S(1)}) custom-call(bf16[128,896]{1,0:T(8,128)(2,1)} %hid_in.1, bf16[64,512]{1,0:T(8,128)(2,1)} %up_in.1, bf16[896,512]{1,0:T(8,128)(2,1)} %w_in.1), custom_call_target="tpu_custom_call" | custom-call | tf_op jit(solution)/shard_map/pallas_call | solution.py:328
  58.2 1.4 %shard_map.51 = (bf16[128,896]{1,0:T(8,128)(2,1)}, f32[896,512]{1,0:T(8,128)}) custom-call(bf16[128,896]{1,0:T(8,128)(2,1)S(1)} %get-tuple-element.4.grad, f32[896,512]{1,0:T(8,128)S(1)} %get-tuple-element.5.weight_grad), custom_call_target="tpu_custom_call" | custom-call | tf_op jit(solution)/shard_map/pallas_call | solution.py:356
